TPU v7x, 32 devices: a whole 2x2x4 slice. The times are simulated.
32 devices in a mesh: shard: 32 (over z, y, x, core).
Axes of the slice: x: 2, y: 2, z: 4, core: 2. Of those that a mesh axis runs over, the one named last changes fastest.
Arguments:
- lookup_ids: int32 [65536], P('shard'), may hold values from 0 to 524287, as said below
- grad_rows: float32 [65536, 128], P('shard'), may hold values from -6 to 6
- emb_table: float32 [524288, 128], P('shard'), may hold values from -4 to 4
- row_accum: float32 [524288], P('shard'), may hold values from 0.01 to 1
Outputs:
- new_table: float32 [524288, 128], P('shard')
- new_accum: float32 [524288], P('shard')
- looked_up: float32 [65536, 128], P('shard')
Inputs may be any that keep to these rules, and one draw needn't show every extreme that they name: `lookup_ids`: each device's 2048 lookups name exactly 64 rows, repeats counted, in the range of every owner; within an owner's range the row numbers follow a power law, so that a few rows are named very often.
All inputs are finite; a program needn't handle non-finite values.
Results may differ from a plain program's by a relative error of at most 0.00002.
Values sent between devices are 32-bit elements; how exact they have to be, the bound alone decides.
A program may use at most 64 MiB of HBM per device.

v0:
```python
import jax
import jax.numpy as jnp
from jax import lax
from jax.sharding import PartitionSpec as P

LEARNING_RATE = 0.5
EPSILON = 1e-08


def on_device(lookup_ids, grad_rows, emb_table, row_accum):
    peer_count = lax.axis_size("shard")
    look_count = lookup_ids.shape[0]
    row_width = grad_rows.shape[1]
    rows_dev = emb_table.shape[0]
    per_peer = look_count // peer_count
    owners = lookup_ids // rows_dev
    offsets = lookup_ids - owners * rows_dev
    arrange = jnp.argsort(owners, stable=True)
    send_offsets = offsets[arrange].astype(jnp.float32).reshape(peer_count, per_peer)
    send_grads = grad_rows[arrange].reshape(peer_count, per_peer, row_width)
    recv_offsets, recv_grads = (
        lax.all_to_all(send_offsets, "shard", split_axis=0, concat_axis=0, tiled=True),
        lax.all_to_all(send_grads, "shard", split_axis=0, concat_axis=0, tiled=True),
    )
    local_rows = recv_offsets.reshape(-1).astype(jnp.int32)
    flat_grads = recv_grads.reshape(-1, row_width)
    summed = jax.ops.segment_sum(flat_grads, local_rows, num_segments=rows_dev)
    new_accum = row_accum + jnp.mean(summed * summed, axis=1)
    new_table = emb_table - LEARNING_RATE * summed / (jnp.sqrt(new_accum)[:, None] + EPSILON)
    fresh_rows = new_table[local_rows].reshape(peer_count, per_peer, row_width)
    returned = lax.all_to_all(fresh_rows, "shard", split_axis=0, concat_axis=0, tiled=True).reshape(
        look_count, row_width
    )
    looked_up = jnp.zeros_like(grad_rows).at[arrange].set(returned)
    return (new_table, new_accum, looked_up)


def solution(mesh):
    in_specs = (P("shard"), P("shard", None), P("shard", None), P("shard"))
    out_specs = (P("shard", None), P("shard"), P("shard", None))
    return jax.shard_map(
        on_device, mesh=mesh, in_specs=in_specs, out_specs=out_specs, check_vma=False
    )
```

profile of v0, /device:TPU:0, one launch (start us, length us, event | category | flops | bytes accessed | tf_op | source)
XLA Modules:
  0.0 140.5 jit_solution(14937994033056056858)
XLA Ops:
  0.6 0.0 copy-start
  0.6 0.8 add_select_fusion
  1.4 5.0 %sort.17 = (s32[2048]{0:T(1024)}, s32[2048]{0:T(1024)S(1)}) sort(s32[2048]{0:T(1024)S(1)} %get-tuple-element.9, s32[2048]{0:T(1024)S(1)} %iota.4), dimensions={0}, to_apply=%region_0.1 | sort | flops 22528 | bytes 32768 | tf_op jit(solution)/shard_map/jit(argsort)/sort | solution.py:18
  6.5 11.8 %gather_fusion = s32[2048]{0:T(1024)S(1)} fusion(s32[2048]{0:T(1024)S(1)} %get-tuple-element.10, s32[2048]{0:T(1024)S(1)} %get-tuple-element.8), kind=kCustom, calls=%fused_computation | custom fusion | bytes 24576 | tf_op jit(solution)/shard_map/gather | solution.py:19
  18.3 0.7 convert_element_type.32
  19.0 7.3 %all-to-all-start = ((f32[32,1,64]{2,1,0:T(1,128)}), f32[32,1,64]{2,1,0:T(1,128)S(1)}, u32[]{:S(2)}, u32[]{:S(2)}) async-start(f32[32,1,64]{2,1,0:T(1,128)} %convert_element_type.32), calls=%async_computation | async-start | bytes 32768 | tf_op jit(solution)/shard_map/all_to_all | solution.py:22
  26.3 0.0 copy-done
  26.3 7.6 %gather_fusion.1 = f32[2048,128]{1,0:T(8,128)} fusion(f32[2048,128]{1,0:T(8,128)S(1)} %copy-done, s32[2048]{0:T(1024)S(1)} %get-tuple-element.8), kind=kCustom, calls=%fused_computation.1 | custom fusion | bytes 2105344 | tf_op jit(solution)/shard_map/gather | solution.py:20
  34.0 0.0 all-to-all-done
  34.0 5.8 %all-to-all-start.1 = ((f32[32,64,128]{2,1,0:T(8,128)}), f32[32,64,128]{2,1,0:T(8,128)S(1)}, u32[]{:S(2)}, u32[]{:S(2)}) async-start(f32[32,64,128]{2,1,0:T(8,128)} %bitcast), calls=%async_computation.1 | async-start | bytes 2097152 | tf_op jit(solution)/shard_map/all_to_all | solution.py:23
  39.8 0.1 convert_reduce_fusion
  39.9 0.1 reshape.92
  39.9 0.1 convert_element_type.34
  40.1 25.9 %all-to-all-done.1 = f32[32,64,128]{2,1,0:T(8,128)S(1)} async-done(((f32[32,64,128]{2,1,0:T(8,128)}), f32[32,64,128]{2,1,0:T(8,128)S(1)}, u32[]{:S(2)}, u32[]{:S(2)}) %all-to-all-start.1) | async-done | bytes 1048608 | tf_op jit(solution)/shard_map/all_to_all | solution.py:23
  66.0 0.0 copy-start.2
  66.0 15.3 %scatter_custom_fusion = f32[16384,128]{1,0:T(8,128)} fusion(s32[2048]{0:T(1024)S(1)} %reshape.92, f32[2048,128]{1,0:T(8,128)S(1)} %bitcast.8, f32[]{:T(128)} %constant.11.clone.1), kind=kCustom, calls=%fused_computation.7 | custom fusion | flops 262144 | bytes 8388612 | tf_op jit(solution)/shard_map/scatter-add | solution.py:27
  81.3 0.0 copy-start.1
  81.3 5.4 %multiply_reduce_fusion = f32[16384]{0:T(1024)S(1)} fusion(f32[16384,128]{1,0:T(8,128)} %scatter_custom_fusion), kind=kLoop, calls=%fused_computation.6 | loop fusion | flops 4177920 | bytes 8454144 | tf_op jit(solution)/shard_map/reduce_sum | solution.py:28
  86.8 0.0 copy-done.2
  86.8 0.6 sqrt_add_fusion
  87.4 0.0 copy-done.1
  87.4 8.0 %divide_subtract_fusion = f32[16384,128]{1,0:T(8,128)} fusion(f32[16384,128]{1,0:T(8,128)} %param.6, f32[16384,128]{1,0:T(8,128)S(1)} %copy-done.1, f32[16384]{0:T(1024)S(1)} %get-tuple-element.5), kind=kLoop, calls=%fused_computation.5 | loop fusion | flops 6291456 | bytes 25231360 | tf_op jit(solution)/shard_map/sub | solution.py:29
  95.4 8.8 %gather_fusion.2 = f32[2048,128]{1,0:T(8,128)S(1)} fusion(f32[16384,128]{1,0:T(8,128)} %divide_subtract_fusion, s32[2048]{0:T(1024)S(1)} %broadcast_clamp_fusion), kind=kCustom, calls=%fused_computation.2 | custom fusion | bytes 2105344 | tf_op jit(solution)/shard_map/gather | solution.py:30
  104.3 29.6 %all_to_all.16 = f32[32,64,128]{2,1,0:T(8,128)S(1)} all-to-all(f32[32,64,128]{2,1,0:T(8,128)S(1)} %bitcast.7), channel_id=1, replica_groups=mesh['shard'=32] {'shard'}, dimensions={0} | all-to-all | bytes 2097152 | tf_op jit(solution)/shard_map/all_to_all | solution.py:31
  133.9 6.6 %scatter_custom_fusion.1 = f32[2048,128]{1,0:T(8,128)} fusion(s32[2048]{0:T(1024)S(1)} %get-tuple-element.7, f32[2048,128]{1,0:T(8,128)S(1)} %bitcast.9, f32[]{:T(128)} %constant.11.clone.1), kind=kCustom, calls=%fused_computation.9 | custom fusion | bytes 1048580 | tf_op jit(solution)/shard_map/scatter | solution.py:34
  (6 shorter events, 0.0 us)
Async XLA Ops:
  0.6 25.7 %copy-start = (f32[2048,128]{1,0:T(8,128)S(1)}, f32[2048,128]{1,0:T(8,128)}, u32[]{:S(2)}) copy-start(f32[2048,128]{1,0:T(8,128)} %param.5) | copy-start | bytes 3145732
  19.0 15.0 %all-to-all-start = ((f32[32,1,64]{2,1,0:T(1,128)}), f32[32,1,64]{2,1,0:T(1,128)S(1)}, u32[]{:S(2)}, u32[]{:S(2)}) async-start(f32[32,1,64]{2,1,0:T(1,128)} %convert_element_type.32), calls=%async_computation | async-start | bytes 32768 | tf_op jit(solution)/shard_map/all_to_all | solution.py:22
  34.0 32.0 %all-to-all-start.1 = ((f32[32,64,128]{2,1,0:T(8,128)}), f32[32,64,128]{2,1,0:T(8,128)S(1)}, u32[]{:S(2)}, u32[]{:S(2)}) async-start(f32[32,64,128]{2,1,0:T(8,128)} %bitcast), calls=%async_computation.1 | async-start | bytes 2097152 | tf_op jit(solution)/shard_map/all_to_all | solution.py:23
  66.0 20.8 %copy-start.2 = (f32[16384]{0:T(1024)S(1)}, f32[16384]{0:T(1024)}, u32[]{:S(2)}) copy-start(f32[16384]{0:T(1024)} %param.7) | copy-start | bytes 196612
  81.3 6.1 %copy-start.1 = (f32[16384,128]{1,0:T(8,128)S(1)}, f32[16384,128]{1,0:T(8,128)}, u32[]{:S(2)}) copy-start(f32[16384,128]{1,0:T(8,128)} %scatter_custom_fusion) | copy-start | bytes 25165828
where the time goes:
time: 141 us; the launch traced here: 140 us
  local copies, waits for them, and re-layouts  35.7 us (25%)
  other arithmetic  35.3 us (25%)
  blocking collectives  29.6 us (21%)
  waiting for transfers between devices  25.9 us (18%)
  starting transfers between devices  13.2 us (9%)
    all_to_all x1, blocking collectives, on_device(): lax.all_to_all(fresh_rows, 'shard', split_axis=0, concat_axis=0, tiled=True)  29.6 us
    all_to_all x1, waiting for transfers between devices, on_device(): lax.all_to_all(send_grads, 'shard', split_axis=0, concat_axis=0, tiled=True)  25.9 us
    scatter-add x1, other arithmetic, on_device(): summed = jax.ops.segment_sum(flat_grads, local_rows, num_segments=rows_dev)  15.3 us
    gather x1, local copies, waits for them, and re-layouts, on_device(): offsets[arrange].astype(jnp.float32).reshape(peer_count, per_peer)  11.8 us
    gather x1, local copies, waits for them, and re-layouts, on_device(): fresh_rows = new_table[local_rows].reshape(peer_count, per_peer, row_width)  8.84 us
    sub x1, other arithmetic, on_device(): emb_table - LEARNING_RATE * summed / (jnp.sqrt(new_accum)[:, None] + EPSI...  7.98 us
    gather x1, local copies, waits for them, and re-layouts, on_device(): send_grads = grad_rows[arrange].reshape(peer_count, per_peer, row_width)  7.64 us
    all_to_all x1, starting transfers between devices, on_device(): lax.all_to_all(send_offsets, 'shard', split_axis=0, concat_axis=0, tiled=...  7.33 us
  transfers between devices with their start and end apart: 2, of which 1 were waited for; matrix products, arithmetic and copies ran while one was open for 6% of the time, Pallas kernels for 0%

commit v1 on v0

v1 whole, which is shorter than its diff:
```python
import functools

import jax
import jax.numpy as jnp
from jax import lax
from jax.experimental import pallas as pl
from jax.experimental.pallas import tpu as pltpu
from jax.sharding import PartitionSpec as P

LEARNING_RATE = 0.5
EPSILON = 1e-08
LANES = 128
MIB = 1024 * 1024
F32 = jnp.float32
BF16 = jnp.bfloat16


def split3(x):
    hi = x.astype(BF16)
    rest = x - hi.astype(F32)
    mid = rest.astype(BF16)
    low = (rest - mid.astype(F32)).astype(BF16)
    return hi, mid, low


def dot(a, b):
    return jnp.dot(a, b, preferred_element_type=F32)


def column_of(row):
    return jnp.transpose(jnp.broadcast_to(row, (LANES, LANES)))


def one_hot_bf16(mask):
    return jnp.where(mask, 1.0, 0.0).astype(BF16)


def arrange_kernel(peers, rows_dev, ids_ref, grads_ref, pos_ref, send_ids_ref, send_ref, terms):
    blocks = ids_ref.shape[0]
    look = blocks * LANES
    per_peer = look // peers
    width = grads_ref.shape[1]
    peer_iota = lax.broadcasted_iota(jnp.int32, (peers, LANES), 0)
    before = one_hot_bf16(
        lax.broadcasted_iota(jnp.int32, (LANES, LANES), 0)
        < lax.broadcasted_iota(jnp.int32, (LANES, LANES), 1)
    )
    base = (per_peer * lax.broadcasted_iota(jnp.int32, (peers, 1), 0)).astype(F32)
    for b in range(blocks):
        ids = ids_ref[b : b + 1, :]
        owner = jnp.zeros_like(ids)
        low = peer_iota * rows_dev
        mine = jnp.where((ids >= low) & (ids < low + rows_dev), 1.0, 0.0)
        rank = dot(mine.astype(BF16), before) + base
        pos_ref[b : b + 1, :] = jnp.sum(mine * rank, axis=0, keepdims=True).astype(jnp.int32)
        base = base + jnp.sum(mine, axis=1, keepdims=True)
    hi, mid, low = split3(grads_ref[...])
    terms[:, 0:width] = hi
    terms[:, width : 2 * width] = mid
    terms[:, 2 * width : 3 * width] = low
    tile = 256
    pos = [pos_ref[b : b + 1, :] for b in range(blocks)]
    per_tile = tile // per_peer

    @pl.loop(0, look // tile)
    def _(t):
        start = pl.multiple_of(t * tile, tile)
        place = start + lax.broadcasted_iota(jnp.int32, (tile, LANES), 0)
        hits = [place == pos[b] for b in range(blocks)]
        pick = jnp.concatenate([one_hot_bf16(h) for h in hits], axis=1)
        out = dot(pick, terms[...])
        send_ref[pl.ds(start, tile), :] = (
            out[:, 0:width] + out[:, width : 2 * width] + out[:, 2 * width : 3 * width]
        )
        named = jnp.zeros((tile, LANES), jnp.int32)
        for b in range(blocks):
            named = named + jnp.where(hits[b], ids_ref[b : b + 1, :], 0)
        named = jnp.sum(named, axis=1, keepdims=True)
        slot = lax.rem(lax.broadcasted_iota(jnp.int32, (tile, LANES), 0), per_peer)
        lane = lax.broadcasted_iota(jnp.int32, (tile, LANES), 1)
        spread = jnp.where(slot == lane, jnp.broadcast_to(named, (tile, LANES)), 0)
        for q in range(per_tile):
            row = jnp.sum(spread[q * per_peer : (q + 1) * per_peer], axis=0, keepdims=True)
            peer = t * per_tile + q
            send_ids_ref[peer] = row - peer * rows_dev


def peer_of(me, step, n):
    return lax.rem(me + n // 2 + step, n)


def meet_all(me, n):
    barrier = pltpu.get_barrier_semaphore()

    def greet(step, carry):
        pl.semaphore_signal(
            barrier,
            inc=1,
            device_id=(lax.rem(me + step, n),),
            device_id_type=pl.DeviceIdType.MESH,
        )
        return carry

    lax.fori_loop(1, n, greet, 0)
    pl.semaphore_wait(barrier, n - 1)


def exchange_kernel(n, count, *refs):
    srcs, dsts = refs[:count], refs[count : 2 * count]
    send_sem, recv_sem, own_sem = refs[2 * count :]
    me = lax.axis_index("shard")
    own = [
        pltpu.make_async_copy(s.at[me], d.at[me], own_sem.at[i])
        for i, (s, d) in enumerate(zip(srcs, dsts))
    ]
    for copy in own:
        copy.start()
    meet_all(me, n)

    def remote(i, step):
        peer = lax.rem(me + step, n)
        return pltpu.make_async_remote_copy(
            src_ref=srcs[i].at[peer],
            dst_ref=dsts[i].at[me],
            send_sem=send_sem.at[i, step],
            recv_sem=recv_sem.at[i, step],
            device_id=(peer,),
            device_id_type=pl.DeviceIdType.MESH,
        )

    half = n // 2
    for i in range(count):

        def start(s, carry, i=i):
            remote(i, half + s).start()

            @pl.when(s > 0)
            def _():
                remote(i, half - s).start()

            return carry

        lax.fori_loop(0, half, start, 0)

    def finish(step, carry):
        for i in range(count):
            source = lax.rem(me - step + n, n)
            pltpu.make_async_remote_copy(
                src_ref=srcs[i].at[source],
                dst_ref=dsts[i].at[source],
                send_sem=send_sem.at[i, step],
                recv_sem=recv_sem.at[i, step],
                device_id=(source,),
                device_id_type=pl.DeviceIdType.MESH,
            ).wait_recv()
        return carry

    lax.fori_loop(1, n, finish, 0)

    def drain(step, carry):
        for i in range(count):
            remote(i, step).wait_send()
        return carry

    lax.fori_loop(1, n, drain, 0)
    for copy in own:
        copy.wait()


def exchange(n, collective_id, *arrays):
    count = len(arrays)
    vmem = pl.BlockSpec(memory_space=pltpu.VMEM)
    return pl.pallas_call(
        functools.partial(exchange_kernel, n, count),
        out_shape=[jax.ShapeDtypeStruct(a.shape, a.dtype) for a in arrays],
        in_specs=[vmem] * count,
        out_specs=[vmem] * count,
        scratch_shapes=[
            pltpu.SemaphoreType.DMA((count, n)),
            pltpu.SemaphoreType.DMA((count, n)),
            pltpu.SemaphoreType.DMA((count,)),
        ],
        compiler_params=pltpu.CompilerParams(
            collective_id=collective_id, has_side_effects=True, vmem_limit_bytes=16 * MIB
        ),
    )(*arrays)


def owner_kernel(
    ids_smem, ids_ref, grads_ref, accum_ref, emb_hbm,
    fresh_ref, new_accum_ref, table_hbm,
    table, terms, weights, hi_hot, lo_hot, in_sem, out_sem,
):
    blocks = ids_ref.shape[0]
    look = blocks * LANES
    width = grads_ref.shape[1]
    groups = accum_ref.shape[0]
    fetch = pltpu.make_async_copy(emb_hbm, table, in_sem)
    fetch.start()
    hi, mid, low = split3(grads_ref[...])
    terms[:, 0:width] = hi
    terms[:, width : 2 * width] = mid
    terms[:, 2 * width : 3 * width] = low
    terms[:, 3 * width : 4 * width] = jnp.ones((look, width), BF16)
    rows = [ids_ref[b : b + 1, :] for b in range(blocks)]
    acc3 = jnp.concatenate(split3(accum_ref[...]), axis=1)
    lane = lax.broadcasted_iota(jnp.int32, (LANES, LANES), 1)
    group_iota = lax.broadcasted_iota(jnp.int32, (LANES, groups), 1)
    fetch.wait()

    @pl.loop(0, blocks)
    def _(b):
        start = pl.multiple_of(b * LANES, LANES)
        here = pl.ds(start, LANES)
        col = column_of(ids_ref[pl.ds(b, 1), :])
        for i in range(LANES):
            fresh_ref[pl.ds(start + i, 1), :] = table[pl.ds(ids_smem[start + i], 1), :]
        same = jnp.concatenate([one_hot_bf16(col == r) for r in rows], axis=1)
        out = dot(same, terms[...])
        summed = out[:, 0:width] + out[:, width : 2 * width] + out[:, 2 * width : 3 * width]
        times = out[:, 3 * width : 3 * width + 1]
        mean = jnp.sum(summed * summed, axis=1, keepdims=True) * (1.0 / width)
        group = lax.shift_right_logical(col, 7)
        at_lane = (col & (LANES - 1)) == lane
        at_group = group[:, 0:1] == group_iota
        found = dot(one_hot_bf16(at_group), acc3)
        found = found[:, 0:LANES] + found[:, LANES : 2 * LANES] + found[:, 2 * LANES : 3 * LANES]
        acc = jnp.sum(jnp.where(at_lane, found, 0.0), axis=1, keepdims=True)
        new_acc = acc + mean
        fresh_ref[here, :] = fresh_ref[here, :] - LEARNING_RATE * summed / (
            jnp.sqrt(new_acc) + EPSILON
        )
        share = jnp.where(at_lane, jnp.broadcast_to(mean / times, (LANES, LANES)), 0.0)
        share_hi, share_mid, share_low = split3(share)
        weights[here, 0:LANES] = share_hi
        weights[here, LANES : 2 * LANES] = share_mid
        weights[here, 2 * LANES : 3 * LANES] = share_low
        hi_hot[here, :] = one_hot_bf16(at_group)

    @pl.loop(0, look // LANES)
    def _(b):
        start = pl.multiple_of(b * LANES, LANES)
        for i in range(LANES):
            table[pl.ds(ids_smem[start + i], 1), :] = fresh_ref[pl.ds(start + i, 1), :]

    store = pltpu.make_async_copy(table, table_hbm, out_sem)
    store.start()
    added = lax.dot_general(
        hi_hot[...], weights[...], (((0,), (0,)), ((), ())), preferred_element_type=F32
    )
    new_accum_ref[...] = accum_ref[...] + (
        added[:, 0:LANES] + added[:, LANES : 2 * LANES] + added[:, 2 * LANES : 3 * LANES]
    )
    store.wait()


def restore_kernel(pos_ref, back_ref, out_ref, terms):
    blocks = pos_ref.shape[0]
    width = back_ref.shape[1]
    hi, mid, low = split3(back_ref[...])
    terms[:, 0:width] = hi
    terms[:, width : 2 * width] = mid
    terms[:, 2 * width : 3 * width] = low
    lane = lax.broadcasted_iota(jnp.int32, (LANES, LANES), 1)

    @pl.loop(0, blocks)
    def _(b):
        col = column_of(pos_ref[pl.ds(b, 1), :])
        pick = jnp.concatenate(
            [one_hot_bf16(col == lane + k * LANES) for k in range(blocks)], axis=1
        )
        out = dot(pick, terms[...])
        out_ref[pl.ds(pl.multiple_of(b * LANES, LANES), LANES), :] = (
            out[:, 0:width] + out[:, width : 2 * width] + out[:, 2 * width : 3 * width]
        )


def on_device(lookup_ids, grad_rows, emb_table, row_accum):
    n = lax.axis_size("shard")
    look, width = grad_rows.shape
    rows_dev = emb_table.shape[0]
    per_peer = look // n
    blocks = look // LANES
    groups = rows_dev // LANES
    vmem = pl.BlockSpec(memory_space=pltpu.VMEM)
    smem = pl.BlockSpec(memory_space=pltpu.SMEM)
    anywhere = pl.BlockSpec(memory_space=pl.ANY)

    pos, send_ids, send = pl.pallas_call(
        functools.partial(arrange_kernel, n, rows_dev),
        out_shape=[
            jax.ShapeDtypeStruct((blocks, LANES), jnp.int32),
            jax.ShapeDtypeStruct((n, 1, LANES), jnp.int32),
            jax.ShapeDtypeStruct((look, width), F32),
        ],
        in_specs=[vmem, vmem],
        out_specs=[vmem] * 3,
        scratch_shapes=[pltpu.VMEM((look, 3 * width), BF16)],
        compiler_params=pltpu.CompilerParams(vmem_limit_bytes=24 * MIB),
    )(lookup_ids.reshape(blocks, LANES), grad_rows)

    recv_ids, recv = exchange(n, 1, send_ids, send.reshape(n, per_peer, width))
    local_ids = recv_ids[:, 0, :per_peer].reshape(look)

    fresh, new_accum, new_table = pl.pallas_call(
        owner_kernel,
        out_shape=[
            jax.ShapeDtypeStruct((look, width), F32),
            jax.ShapeDtypeStruct((groups, LANES), F32),
            jax.ShapeDtypeStruct((rows_dev, width), F32),
        ],
        in_specs=[smem, vmem, vmem, vmem, anywhere],
        out_specs=[vmem, vmem, anywhere],
        scratch_shapes=[
            pltpu.VMEM((rows_dev, width), F32),
            pltpu.VMEM((look, 4 * width), BF16),
            pltpu.VMEM((look, 3 * LANES), BF16),
            pltpu.VMEM((look, groups), BF16),
            pltpu.VMEM((8, LANES), BF16),
            pltpu.SemaphoreType.DMA(()),
            pltpu.SemaphoreType.DMA(()),
        ],
        compiler_params=pltpu.CompilerParams(vmem_limit_bytes=36 * MIB),
    )(
        local_ids,
        local_ids.reshape(blocks, LANES),
        recv.reshape(look, width),
        row_accum.reshape(groups, LANES),
        emb_table,
    )

    (back,) = exchange(n, 2, fresh.reshape(n, per_peer, width))

    looked_up = pl.pallas_call(
        restore_kernel,
        out_shape=jax.ShapeDtypeStruct((look, width), F32),
        in_specs=[vmem, vmem],
        out_specs=vmem,
        scratch_shapes=[pltpu.VMEM((look, 3 * width), BF16)],
        compiler_params=pltpu.CompilerParams(vmem_limit_bytes=24 * MIB),
    )(pos, back.reshape(look, width))
    return (new_table, new_accum.reshape(rows_dev), looked_up)


def solution(mesh):
    in_specs = (P("shard"), P("shard", None), P("shard", None), P("shard"))
    out_specs = (P("shard", None), P("shard"), P("shard", None))
    return jax.shard_map(
        on_device, mesh=mesh, in_specs=in_specs, out_specs=out_specs, check_vma=False
    )
```

time: 141 us -> 102 us (0.72)
  Pallas kernels: 0 us -> 94.7 us
  other arithmetic: 35.3 us -> 0 us
  blocking collectives: 29.6 us -> 0 us
  local copies, waits for them, and re-layouts: 35.7 us -> 6.33 us
  waiting for transfers between devices: 25.9 us -> 0 us
  starting transfers between devices: 13.2 us -> 0 us
    pallas_call x0 -> x5, Pallas kernels: none -> 94.7 us  [the longest x2 61 us: exchange(): pl.pallas_call(functools.partial(exchange_kernel, n, count), out_shape=[j...]
    all_to_all x1 -> x0, blocking collectives: 29.6 us -> none  [on_device(): lax.all_to_all(fresh_rows, 'shard', split_axis=0, concat_axis=0, tiled=True)]
    gather x3 -> x0, local copies, waits for them, and re-layouts: 28.2 us -> none  [the longest x1 11.8 us: on_device(): offsets[arrange].astype(jnp.float32).reshape(peer_count, per_peer)]
    all_to_all x2 -> x0, waiting for transfers between devices: 25.9 us -> none  [the longest x1 25.9 us: on_device(): lax.all_to_all(send_grads, 'shard', split_axis=0, concat_axis=0, tiled=True)]
    scatter-add x1 -> x0, other arithmetic: 15.3 us -> none  [on_device(): summed = jax.ops.segment_sum(flat_grads, local_rows, num_segments=rows_dev)]
    all_to_all x2 -> x0, starting transfers between devices: 13.2 us -> none  [the longest x1 7.33 us: on_device(): lax.all_to_all(send_offsets, 'shard', split_axis=0, concat_axis=0, tiled=...]
    sub x1 -> x0, other arithmetic: 7.98 us -> none  [on_device(): emb_table - LEARNING_RATE * summed / (jnp.sqrt(new_accum)[:, None] + EPSI...]
    scatter x1 -> x0, local copies, waits for them, and re-layouts: 6.57 us -> none  [on_device(): looked_up = jnp.zeros_like(grad_rows).at[arrange].set(returned)]
  transfers between devices with their start and end apart: 2 -> 0, of which waited for: 1 -> 0; matrix products, arithmetic and copies ran while one was open for 6% -> 0% of each run, Pallas kernels for 0% -> 0%
where the time goes in v1:
time: 102 us
  Pallas kernels  94.7 us (93%)
  local copies, waits for them, and re-layouts  6.33 us (6%)
    pallas_call x2, Pallas kernels, exchange(): pl.pallas_call(functools.partial(exchange_kernel, n, count), out_shape=[j...  61 us
    pallas_call x1, Pallas kernels, on_device(): pl.pallas_call(owner_kernel, out_shape=[jax.ShapeDtypeStruct((look, width...  17.7 us
    pallas_call x1, Pallas kernels, on_device(): pl.pallas_call(restore_kernel, out_shape=jax.ShapeDtypeStruct((look, widt...  9.34 us
    pallas_call x1, Pallas kernels, on_device(): pl.pallas_call(functools.partial(arrange_kernel, n, rows_dev), out_shape=...  6.62 us
    unnamed x8, local copies, waits for them, and re-layouts  6.14 us

profile of v1, /device:TPU:0, one launch (start us, length us, event | category | flops | bytes accessed | tf_op | source)
XLA Modules:
  0.0 101.7 jit_solution(4247250198591570620)
XLA Ops:
  0.6 0.0 copy-start.1
  0.6 1.2 %copy-done.1 = f32[2048,128]{1,0:T(8,128)S(1)} copy-done((f32[2048,128]{1,0:T(8,128)S(1)}, f32[2048,128]{1,0:T(8,128)}, u32[]{:S(2)}) %copy-start.1) | copy-done | bytes 1048600
  1.9 0.0 copy-start.3
  1.9 0.7 copy-done.3
  2.6 6.6 %shard_map.67 = (s32[16,128]{1,0:T(8,128)S(1)}, s32[32,1,128]{2,1,0:T(1,128)S(1)}, f32[2048,128]{1,0:T(8,128)S(1)}) custom-call(s32[16,128]{1,0:T(8,128)S(1)} %bitcast.13, f32[2048,128]{1,0:T(8,128)S(1)} %copy-done.1), custom_call_target="tpu_custom_call" | custom-call | tf_op jit(solution)/shard_map/pallas_call | solution.py:289
  9.2 32.0 %shard_map.68 = (s32[32,1,128]{2,1,0:T(1,128)S(1)}, f32[32,64,128]{2,1,0:T(8,128)S(1)}) custom-call(s32[32,1,128]{2,1,0:T(1,128)S(1)} %get-tuple-element.11.refs_0_, f32[32,64,128]{2,1,0:T(8,128)S(1)} %bitcast.11), custom_call_target="tpu_custom_call" | custom-call | tf_op jit(solution)/shard_map/pallas_call | solution.py:173
  41.2 0.1 fusion
  41.2 0.1 reshape_reshape_squeeze.3.ids_ref
  41.3 0.1 reshape_squeeze.3.ids_smem
  41.4 0.0 copy-start
  41.4 3.4 %copy-done = f32[16384,128]{1,0:T(8,128)S(1)} copy-done((f32[16384,128]{1,0:T(8,128)S(1)}, f32[16384,128]{1,0:T(8,128)}, u32[]{:S(2)}) %copy-start) | copy-done | bytes 8388632
  44.7 0.0 copy-start.2
  44.7 0.8 copy-done.2
  45.6 17.7 %shard_map.69 = (f32[2048,128]{1,0:T(8,128)S(1)}, f32[128,128]{1,0:T(8,128)}, f32[16384,128]{1,0:T(8,128)}) custom-call(s32[2048]{0:T(1024)S(1)} %reshape_squeeze.3.ids_smem, s32[16,128]{1,0:T(8,128)S(1)} %reshape_reshape_squeeze.3.ids_ref, f32[2048,128]{1,0:T(8,128)S(1)} %bitcast.9, f32[128,128]{1,0:T(8,128)S(1)} %bitcast.12, f32[16384,128]{1,0:T(8,128)S(1)} %copy-done), custom_call_target="tpu_custom_call" | custom-call | tf_op jit(solution)/shard_map/pallas_call | solution.py:305
  63.3 29.0 %shard_map.70 = f32[32,64,128]{2,1,0:T(8,128)S(1)} custom-call(f32[32,64,128]{2,1,0:T(8,128)S(1)} %bitcast.10), custom_call_target="tpu_custom_call" | custom-call | tf_op jit(solution)/shard_map/pallas_call | solution.py:173
  92.3 9.3 %shard_map.71 = f32[2048,128]{1,0:T(8,128)} custom-call(s32[16,128]{1,0:T(8,128)S(1)} %get-tuple-element.17.pos_ref, f32[2048,128]{1,0:T(8,128)S(1)} %bitcast.8), custom_call_target="tpu_custom_call" | custom-call | tf_op jit(solution)/shard_map/pallas_call | solution.py:334
Async XLA Ops:
  0.6 1.2 %copy-start.1 = (f32[2048,128]{1,0:T(8,128)S(1)}, f32[2048,128]{1,0:T(8,128)}, u32[]{:S(2)}) copy-start(f32[2048,128]{1,0:T(8,128)} %grads_ref.1) | copy-start | bytes 3145732
  1.9 0.7 copy-start.3
  41.4 3.4 %copy-start = (f32[16384,128]{1,0:T(8,128)S(1)}, f32[16384,128]{1,0:T(8,128)}, u32[]{:S(2)}) copy-start(f32[16384,128]{1,0:T(8,128)} %emb_hbm.1) | copy-start | bytes 25165828
  44.7 0.8 copy-start.2
